TPU v7x, 32 devices: a 4x4x1 block of a 4x4x8 slice. The times are simulated.
32 devices in a mesh: dp: 1 (over z), ep: 32 (over y, x, core).
Axes of the slice: x: 4, y: 4, z: 1, core: 2. Of those that a mesh axis runs over, the one named last changes fastest.
The devices are a block of a 4x4x8 slice.
Arguments:
- x_rows: bfloat16 [32768, 2048], P(('dp', 'ep'))
- logits: float32 [32768, 256], P(('dp', 'ep'))
- w_in: bfloat16 [256, 2048, 512], P('ep')
- w_out: bfloat16 [256, 512, 2048], P('ep')
Outputs:
- output: bfloat16 [32768, 2048], P(('dp', 'ep'))
All inputs are finite; a program needn't handle non-finite values.
Results may differ from a plain program's by a relative error of at most 0.001.
Values are sent between devices in bfloat16 or wider.
A program may use at most 768 MiB of HBM per device.

v0:
```python
import jax
import jax.numpy as jnp
from jax import lax
from jax.sharding import PartitionSpec as P

CAP_FACTOR = 2


def solution(mesh):
    group_size = mesh.shape['ep']
    row_spec = P(('dp', 'ep'), None)
    expert_spec = P('ep', None, None)

    def local_step(x_rows, logits, w_in, w_out):
        tok_dev, d_model = x_rows.shape
        experts = logits.shape[1]
        exp_dev = w_in.shape[0]
        capacity = CAP_FACTOR * tok_dev * group_size // experts
        src_cap = 4 * tok_dev // experts
        my_index = lax.axis_index('ep')
        gate_probs = jax.nn.softmax(logits, axis=-1)
        top_vals, top_ids = lax.top_k(logits, 2)
        chosen = (logits >= top_vals[:, 1:2]).astype(jnp.int32)
        local_before = jnp.cumsum(chosen, axis=0) - chosen
        local_counts = jnp.sum(chosen, axis=0).astype(jnp.float32)
        all_counts = lax.all_gather(local_counts, 'ep').astype(jnp.int32)
        dev_offsets = jnp.cumsum(all_counts, axis=0) - all_counts
        local_pos = jnp.take_along_axis(local_before, top_ids, axis=1)
        kept_mask = local_pos + jnp.take(dev_offsets[my_index], top_ids) < capacity
        send_row = jnp.where(kept_mask, top_ids * src_cap + local_pos, experts * src_cap)
        tok_ids = jnp.broadcast_to(jnp.arange(tok_dev, dtype=jnp.int32)[:, None], (tok_dev, 2))
        slot_tok = jnp.full((experts * src_cap,), tok_dev, jnp.int32).at[send_row.reshape(-1)].set(tok_ids.reshape(-1), mode='drop')
        send_buf = jnp.take(x_rows, slot_tok, axis=0, mode='fill', fill_value=0)
        recv_buf = lax.all_to_all(send_buf, 'ep', 0, 0, tiled=True)

        own_counts = lax.dynamic_slice_in_dim(all_counts, my_index * exp_dev, exp_dev, axis=1)
        own_offsets = lax.dynamic_slice_in_dim(dev_offsets, my_index * exp_dev, exp_dev, axis=1)
        kept_counts = jnp.minimum(jnp.maximum(capacity - own_offsets, 0), own_counts)
        slot_ends = (own_offsets + kept_counts).T
        cap_ids = jnp.arange(capacity, dtype=jnp.int32)
        below_mask = slot_ends[:, None, :] <= cap_ids[None, :, None]
        src_dev = jnp.sum(below_mask.astype(jnp.int32), axis=2)
        slot_start = jnp.sum(jnp.where(below_mask, kept_counts.T[:, None, :], 0), axis=2)
        exp_local = jnp.arange(exp_dev, dtype=jnp.int32)
        recv_row = (src_dev * exp_dev + exp_local[:, None]) * src_cap + cap_ids[None, :] - slot_start
        recv_row = jnp.where(src_dev < group_size, recv_row, group_size * exp_dev * src_cap)
        expert_rows = jnp.take(recv_buf, recv_row.reshape(-1), axis=0, mode='fill', fill_value=0).reshape(exp_dev, capacity, d_model)
        hidden = jax.nn.gelu(jnp.einsum('ecd,edf->ecf', expert_rows, w_in, preferred_element_type=jnp.float32), approximate=True).astype(jnp.bfloat16)
        expert_out = jnp.einsum('ecf,efd->ecd', hidden, w_out, preferred_element_type=jnp.float32).astype(jnp.bfloat16).reshape(exp_dev * capacity, d_model)

        src_slots = jnp.arange(src_cap, dtype=jnp.int32)
        back_row = exp_local[None, :, None] * capacity + own_offsets[:, :, None] + src_slots[None, None, :]
        back_row = jnp.where(src_slots[None, None, :] < kept_counts[:, :, None], back_row, exp_dev * capacity)
        back_buf = jnp.take(expert_out, back_row.reshape(-1), axis=0, mode='fill', fill_value=0)
        ret_buf = lax.all_to_all(back_buf, 'ep', 0, 0, tiled=True)

        rows_back = jnp.take(ret_buf, send_row, axis=0, mode='fill', fill_value=0)
        pick_gate = jnp.take_along_axis(gate_probs, top_ids, axis=1)
        mix_sum = jnp.sum(pick_gate[:, :, None] * rows_back.astype(jnp.float32), axis=1)
        return (x_rows.astype(jnp.float32) + mix_sum).astype(jnp.bfloat16)

    return jax.shard_map(local_step, mesh=mesh, in_specs=(row_spec, row_spec, expert_spec, expert_spec), out_specs=row_spec, check_vma=False)
```

profile of v0, /device:TPU:107, one launch (start us, length us, event | category | flops | bytes accessed | tf_op | source)
XLA Modules:
  0.0 938.6 jit_solution(15560441855086507099)
XLA Ops:
  0.0 166.0 %top_k.7 = (f32[1024,2]{1,0:T(8,128)S(1)}, s32[1024,2]{1,0:T(8,128)S(1)}) custom-call(f32[1024,256]{1,0:T(8,128)} %param.5), custom_call_target="TopK", called_computations={%compare_greater_than.1.1.clone.clone} | custom-call | tf_op jit(solution)/shard_map/top_k | solution.py:22
  166.3 0.9 reshape.342
  167.2 0.4 slice_reduce_fusion
  167.5 0.9 reshape.326
  168.7 2.4 fusion.36
  171.1 27.9 %all-gather.1 = f32[32,1,256]{2,1,0:T(1,128)S(1)} all-gather(f32[1,1,256]{2,1,0:T(1,128)S(1)} %bitcast.58), channel_id=2, replica_groups=mesh['dp'=1,'ep'=32] {'ep'}, dimensions={0}, use_global_device_ids=true | all-gather | bytes 33792 | tf_op jit(solution)/shard_map/all_gather | solution.py:26
  199.0 0.6 copy_convert_fusion
  199.7 13.1 %gather_fusion = s32[2048]{0:T(1024)S(1)} fusion(s32[256]{0:T(256)S(1)} %bitcast.47, s32[2048]{0:T(1024)S(1)} %broadcast_clamp_fusion.3), kind=kCustom, calls=%fused_computation | custom fusion | bytes 24576 | tf_op jit(solution)/shard_map/jit(_take)/gather | solution.py:29
  212.9 1.3 reshape.287
  214.1 0.6 fusion.21
  215.5 16.6 %gather_fusion.6 = s32[2048]{0:T(1024)S(1)} fusion(s32[1024,256]{1,0:T(8,128)S(1)} %bitcast_subtract_fusion, s32[2048]{0:T(1024)S(1)} %copy-done.1), kind=kCustom, calls=%fused_computation.6 | custom fusion | bytes 32768 | tf_op jit(solution)/shard_map/jit(take_along_axis)/gather | solution.py:28
  232.1 0.5 reshape.335
  232.6 1.0 compare_and_fusion
  234.0 8.2 scatter_custom_fusion
  242.2 34.1 %gather_fusion.1 = bf16[4096,2048]{1,0:T(8,128)(2,1)} fusion(bf16[1024,2048]{1,0:T(8,128)(2,1)} %param.4, s32[4096]{0:T(1024)S(1)} %fusion.25), kind=kCustom, calls=%fused_computation.1 | custom fusion | bytes 33570816 | tf_op jit(solution)/shard_map/jit(_take)/gather | solution.py:33
  276.3 14.0 %broadcast_select_fusion = bf16[32,128,2048]{2,1,0:T(8,128)(2,1)} fusion(bf16[32,128,2048]{2,1,0:T(8,128)(2,1)} %bitcast.50, pred[32,128]{1,0:T(8,128)(4,1)S(1)} %and_bitcast_fusion), kind=kLoop, calls=%fused_computation.9 | loop fusion | flops 8388608 | bytes 33558528 | tf_op jit(solution)/shard_map/jit(_take)/select_n | solution.py:33
  290.3 12.8 %all-to-all-start = ((bf16[32,128,2048]{2,1,0:T(8,128)(2,1)}), bf16[32,128,2048]{2,1,0:T(8,128)(2,1)}, u32[]{:S(2)}, u32[]{:S(2)}) async-start(bf16[32,128,2048]{2,1,0:T(8,128)(2,1)} %broadcast_select_fusion), calls=%async_computation | async-start | bytes 33554432 | tf_op jit(solution)/shard_map/all_to_all | solution.py:34
  304.2 222.7 %all-to-all-done = bf16[32,128,2048]{2,1,0:T(8,128)(2,1)} async-done(((bf16[32,128,2048]{2,1,0:T(8,128)(2,1)}), bf16[32,128,2048]{2,1,0:T(8,128)(2,1)}, u32[]{:S(2)}, u32[]{:S(2)}) %all-to-all-start) | async-done | bytes 16777248 | tf_op jit(solution)/shard_map/all_to_all | solution.py:34
  526.9 24.3 %gather_fusion.2 = bf16[2048,2048]{1,0:T(8,128)(2,1)} fusion(bf16[4096,2048]{1,0:T(8,128)(2,1)} %bitcast.16, s32[2048]{0:T(1024)S(1)} %broadcast_clamp_fusion.2), kind=kCustom, calls=%fused_computation.2 | custom fusion | bytes 16785408 | tf_op jit(solution)/shard_map/jit(_take)/gather | solution.py:47
  551.1 25.9 %convolution_convert_fusion = bf16[8,256,2048]{2,1,0:T(8,128)(2,1)} fusion(bf16[8,512,2048]{2,1,0:T(8,128)(2,1)} %param.7, bf16[8,2048,512]{2,1,0:T(8,128)(2,1)} %param.6, bf16[8,256,2048]{2,1,0:T(8,128)(2,1)} %bitcast.52, pred[8,256]{1,0:T(8,128)(4,1)S(1)} %compare_and_fusion.3), kind=kOutput, calls=%fused_computation.17 | convolution fusion | flops 8607760384 | bytes 50333696 | tf_op jit(solution)/shard_map/ecf,efd->ecd/dot_general | solution.py:49
  577.0 35.8 %gather_fusion.3 = bf16[4096,2048]{1,0:T(8,128)(2,1)} fusion(bf16[2048,2048]{1,0:T(8,128)(2,1)} %bitcast.48, s32[4096]{0:T(1024)S(1)} %broadcast_clamp_fusion), kind=kCustom, calls=%fused_computation.3 | custom fusion | bytes 33570816 | tf_op jit(solution)/shard_map/jit(_take)/gather | solution.py:54
  612.8 14.0 %broadcast_select_fusion.1 = bf16[32,128,2048]{2,1,0:T(8,128)(2,1)} fusion(bf16[32,128,2048]{2,1,0:T(8,128)(2,1)} %bitcast.49, pred[32,128]{1,0:T(8,128)(4,1)S(1)} %copy.25), kind=kLoop, calls=%fused_computation.10 | loop fusion | flops 8388608 | bytes 33558528 | tf_op jit(solution)/shard_map/jit(_take)/select_n | solution.py:54
  626.8 4.4 all-to-all-start.1
  631.4 0.4 fusion.24
  631.8 0.3 fusion.23
  632.2 16.6 %gather_fusion.5 = f32[2048]{0:T(1024)S(1)} fusion(f32[1024,256]{1,0:T(8,128)S(1)} %fusion.23, s32[2048]{0:T(1024)S(1)} %copy-done.2), kind=kCustom, calls=%fused_computation.5 | custom fusion | bytes 32768 | tf_op jit(solution)/shard_map/jit(take_along_axis)/gather | solution.py:58
  648.8 0.5 reshape.329
  649.8 203.8 %all-to-all-done.1 = bf16[32,128,2048]{2,1,0:T(8,128)(2,1)} async-done(((bf16[32,128,2048]{2,1,0:T(8,128)(2,1)}), bf16[32,128,2048]{2,1,0:T(8,128)(2,1)}, u32[]{:S(2)}, u32[]{:S(2)}) %all-to-all-start.1) | async-done | bytes 16777248 | tf_op jit(solution)/shard_map/all_to_all | solution.py:55
  853.6 24.3 %gather_fusion.4 = bf16[2048,2048]{1,0:T(8,128)(2,1)} fusion(bf16[4096,2048]{1,0:T(8,128)(2,1)} %bitcast.22, s32[2048]{0:T(1024)S(1)} %broadcast_clamp_fusion.1), kind=kCustom, calls=%fused_computation.4 | custom fusion | bytes 16785408 | tf_op jit(solution)/shard_map/jit(_take)/gather | solution.py:57
  877.8 14.1 %reshape.319 = bf16[1024,2,2048]{2,1,0:T(2,128)(2,1)} reshape(bf16[2048,2048]{1,0:T(8,128)(2,1)} %gather_fusion.4) | data formatting | bytes 16777216 | tf_op jit(solution)/shard_map/jit(_take)/gather | solution.py:57
  892.0 39.6 %multiply_reduce_fusion = f32[1024,2048]{1,0:T(8,128)} fusion(bf16[1024,2,2048]{2,1,0:T(2,128)(2,1)} %reshape.319, pred[1024,2]{1,0:T(8,128)(4,1)S(1)} %copy-done.11, f32[1024,2]{1,0:T(8,128)S(1)} %broadcast_select_fusion.3), kind=kLoop, calls=%fused_computation.8 | loop fusion | flops 14680064 | bytes 16787456 | tf_op jit(solution)/shard_map/reduce_sum | solution.py:59
  931.5 7.1 add_convert_fusion
  (71 shorter events, 3.3 us)
Async XLA Ops:
  166.0 2.4 copy-start.5
  199.7 13.2 %copy-start.12 = (s32[32,256]{1,0:T(8,128)}, s32[32,256]{1,0:T(8,128)S(1)}, u32[]{:S(2)}) copy-start(s32[32,256]{1,0:T(8,128)S(1)} %bitcast_subtract_fusion.1) | copy-start | bytes 98308
  199.7 14.4 %copy-start.4 = (s32[1024,256]{1,0:T(8,128)S(1)}, s32[1024,256]{1,0:T(8,128)}, u32[]{:S(2)}) copy-start(s32[1024,256]{1,0:T(8,128)} %get-tuple-element.20) | copy-start | bytes 3145732
  212.9 2.6 copy-start.1
  215.5 17.2 %copy-start.6 = (s32[1024,2]{1,0:T(8,128)S(1)}, s32[1024,2]{1,0:T(8,128)}, u32[]{:S(2)}) copy-start(s32[1024,2]{1,0:T(8,128)} %copy-done.5) | copy-start | bytes 24580
  215.5 17.2 %copy-start.10 = (s32[1024,2]{1,0:T(8,128)S(1)}, s32[1024,2]{1,0:T(8,128)}, u32[]{:S(2)}) copy-start(s32[1024,2]{1,0:T(8,128)} %reshape.287) | copy-start | bytes 24580
  233.6 42.7 %copy-start.8 = (s32[1024,2]{1,0:T(8,128)}, s32[1024,2]{1,0:T(8,128)S(1)}, u32[]{:S(2)}) copy-start(s32[1024,2]{1,0:T(8,128)S(1)} %get-tuple-element.16) | copy-start | bytes 24580
  290.3 12.9 %copy-start.13 = (s32[32,256]{1,0:T(8,128)S(1)}, s32[32,256]{1,0:T(8,128)}, u32[]{:S(2)}) copy-start(s32[32,256]{1,0:T(8,128)} %copy-done.12) | copy-start | bytes 98308
  290.3 12.9 %copy-start.14 = (s32[32,1,256]{2,0,1:T(8,128)S(1)}, s32[32,1,256]{2,0,1:T(8,128)}, u32[]{:S(2)}) copy-start(s32[32,1,256]{2,0,1:T(8,128)} %get-tuple-element.22) | copy-start | bytes 98308
  290.3 236.6 %all-to-all-start = ((bf16[32,128,2048]{2,1,0:T(8,128)(2,1)}), bf16[32,128,2048]{2,1,0:T(8,128)(2,1)}, u32[]{:S(2)}, u32[]{:S(2)}) async-start(bf16[32,128,2048]{2,1,0:T(8,128)(2,1)} %broadcast_select_fusion), calls=%async_computation | async-start | bytes 33554432 | tf_op jit(solution)/shard_map/all_to_all | solution.py:34
  626.8 4.4 copy-start.3
  626.8 5.4 copy-start.2
  626.8 226.8 %all-to-all-start.1 = ((bf16[32,128,2048]{2,1,0:T(8,128)(2,1)}), bf16[32,128,2048]{2,1,0:T(8,128)(2,1)}, u32[]{:S(2)}, u32[]{:S(2)}) async-start(bf16[32,128,2048]{2,1,0:T(8,128)(2,1)} %broadcast_select_fusion.1), calls=%async_computation.1 | async-start | bytes 33554432 | tf_op jit(solution)/shard_map/all_to_all | solution.py:55
  632.2 17.2 %copy-start.9 = (s32[1024,2]{1,0:T(8,128)S(1)}, s32[1024,2]{1,0:T(8,128)}, u32[]{:S(2)}) copy-start(s32[1024,2]{1,0:T(8,128)} %copy-done.8) | copy-start | bytes 24580
  632.2 17.5 %copy-start.7 = (s32[1024,2]{1,0:T(8,128)S(1)}, s32[1024,2]{1,0:T(8,128)}, u32[]{:S(2)}) copy-start(s32[1024,2]{1,0:T(8,128)} %copy-done.5) | copy-start | bytes 24580
  877.8 14.1 %copy-start.11 = (pred[1024,2]{1,0:T(8,128)(4,1)S(1)}, pred[1024,2]{1,0:T(8,128)(4,1)}, u32[]{:S(2)}) copy-start(pred[1024,2]{1,0:T(8,128)(4,1)} %get-tuple-element.15) | copy-start | bytes 6148
  891.9 39.6 %copy-start = (bf16[1024,2048]{1,0:T(8,128)(2,1)S(1)}, bf16[1024,2048]{1,0:T(8,128)(2,1)}, u32[]{:S(2)}) copy-start(bf16[1024,2048]{1,0:T(8,128)(2,1)} %param.4) | copy-start | bytes 12582916
where the time goes:
time: 940 us; the launch traced here: 939 us
  waiting for transfers between devices  426 us (45%)
  other arithmetic  248 us (26%)
  local copies, waits for them, and re-layouts  193 us (21%)
  blocking collectives  27.9 us (3%)
  matrix products  25.9 us (3%)
  starting transfers between devices  17.3 us (2%)
    all_to_all x1, waiting for transfers between devices, local_step(): recv_buf = lax.all_to_all(send_buf, 'ep', 0, 0, tiled=True)  223 us
    all_to_all x1, waiting for transfers between devices, local_step(): ret_buf = lax.all_to_all(back_buf, 'ep', 0, 0, tiled=True)  204 us
    top_k x1, other arithmetic, local_step(): top_vals, top_ids = lax.top_k(logits, 2)  166 us
    reduce_sum x1, other arithmetic, local_step(): jnp.sum(pick_gate[:, :, None] * rows_back.astype(jnp.float32), axis=1)  39.6 us
    gather x2, local copies, waits for them, and re-layouts, local_step(): rows_back = jnp.take(ret_buf, send_row, axis=0, mode='fill', fill_value=0)  38.4 us
    gather x1, local copies, waits for them, and re-layouts, local_step(): jnp.take(expert_out, back_row.reshape(-1), axis=0, mode='fill', fill_valu...  35.8 us
    gather x1, local copies, waits for them, and re-layouts, local_step(): send_buf = jnp.take(x_rows, slot_tok, axis=0, mode='fill', fill_value=0)  34.1 us
    all_gather x1, blocking collectives, local_step(): all_counts = lax.all_gather(local_counts, 'ep').astype(jnp.int32)  27.9 us
  transfers between devices with their start and end apart: 2, of which 2 were waited for; matrix products, arithmetic and copies ran while one was open for 2% of the time, Pallas kernels for 0%

commit v1 on v0

v1 whole, which is shorter than its diff:
```python
import functools

import jax
import jax.numpy as jnp
from jax import lax
from jax.experimental import pallas as pl
from jax.experimental.pallas import tpu as pltpu
from jax.sharding import PartitionSpec as P

CAP_FACTOR = 2
SLOT_FACTOR = 4
CORES = 2
SUB = 16
LANE = 128
VMEM_LIMIT = 62 * 1024 * 1024
BF16 = jnp.bfloat16
F32 = jnp.float32
I32 = jnp.int32


def iota(shape, dim):
    return lax.broadcasted_iota(I32, shape, dim)


def route_kernel(logits_ref, tok_ref, gate_ref, count_ref):
    tokens, experts = logits_ref.shape
    lt = logits_ref[...].T
    ids = iota(lt.shape, 0)
    m1 = jnp.max(lt, axis=0, keepdims=True)
    e1 = jnp.min(jnp.where(lt == m1, ids, experts), axis=0, keepdims=True)
    rest = jnp.where(ids == e1, -jnp.inf, lt)
    m2 = jnp.max(rest, axis=0, keepdims=True)
    e2 = jnp.min(jnp.where(rest == m2, ids, experts), axis=0, keepdims=True)
    total = jnp.sum(jnp.exp(lt - m1), axis=0, keepdims=True)
    hit1 = ids == e1
    hit2 = ids == e2
    chosen = jnp.where(hit1 | hit2, 1.0, 0.0).astype(BF16)
    upper = jnp.where(iota((tokens, tokens), 0) < iota((tokens, tokens), 1), 1.0, 0.0).astype(BF16)
    before = jnp.dot(chosen, upper, preferred_element_type=F32)
    pos1 = jnp.sum(jnp.where(hit1, before, 0.0), axis=0, keepdims=True)
    pos2 = jnp.sum(jnp.where(hit2, before, 0.0), axis=0, keepdims=True)
    tok_ref[0:1, :] = e1
    tok_ref[1:2, :] = e2
    tok_ref[2:3, :] = pos1.astype(I32)
    tok_ref[3:4, :] = pos2.astype(I32)
    gate_ref[0:1, :] = 1.0 / total
    gate_ref[1:2, :] = jnp.exp(m2 - m1) / total
    ones = jnp.ones((8, tokens), BF16)
    count_ref[...] = lax.dot_general(ones, chosen, (((1,), (1,)), ((), ())), preferred_element_type=F32)


def plan_kernel(sizes, capacity, exp_dev, me_ref, counts_ref, tok_ref, gate_ref,
                row_ref, keep_ref, start_ref, cnt_ref, pick_ref):
    devs, experts = counts_ref.shape
    tokens = tok_ref.shape[1]
    exp_chip = CORES * exp_dev
    me = me_ref[0]
    chip = me // CORES
    core = me % CORES
    counts = counts_ref[...]
    lower = jnp.where(iota((devs, devs), 1) < iota((devs, devs), 0), 1.0, 0.0).astype(BF16)
    offs = jnp.dot(lower, counts.astype(BF16), preferred_element_type=F32)
    kept = jnp.minimum(jnp.maximum(capacity - offs, 0.0), counts)
    kept_b = kept.astype(BF16)
    row_e = iota((experts, experts), 0)
    col_e = iota((experts, experts), 1)
    same = (row_e // exp_chip == col_e // exp_chip) & (row_e < col_e)
    start = jnp.dot(kept_b, jnp.where(same, 1.0, 0.0).astype(BF16), preferred_element_type=F32)
    start_b = start.astype(BF16)
    member = jnp.where(iota((experts, LANE), 0) // exp_chip == iota((experts, LANE), 1), 1.0, 0.0).astype(BF16)
    totals = jnp.dot(kept_b, member, preferred_element_type=F32)
    most = jnp.max(jnp.max(totals, axis=0, keepdims=True), axis=1, keepdims=True).astype(I32)
    size = jnp.full((1, 1), sizes[0], I32)
    pick = jnp.zeros((1, 1), I32)
    for small, large in zip(sizes[:-1], sizes[1:]):
        size = jnp.where(most > small, large, size)
        pick = pick + jnp.where(most > small, 1, 0)
    pick_ref[...] = jnp.broadcast_to(pick, pick_ref.shape)

    mine = iota((devs, experts), 0) == me
    my_start = jnp.sum(jnp.where(mine, start, 0.0), axis=0, keepdims=True)
    my_kept = jnp.sum(jnp.where(mine, kept, 0.0), axis=0, keepdims=True)
    look = jnp.concatenate([my_start, my_kept, jnp.zeros((6, experts), F32)], axis=0).astype(BF16)
    ids = iota((experts, tokens), 0)
    lanes = experts // exp_chip
    for k in range(2):
        e = tok_ref[k:k + 1, :]
        pos = tok_ref[2 + k:3 + k, :]
        hit = jnp.where(ids == e, 1.0, 0.0).astype(BF16)
        got = jnp.dot(look, hit, preferred_element_type=F32).astype(I32)
        keep = pos < got[1:2, :]
        row = (e // exp_chip) * size + got[0:1, :] + pos
        row_ref[k:k + 1, :] = jnp.where(keep, row, lanes * size)
        keep_ref[k:k + 1, :] = jnp.where(keep, gate_ref[k:k + 1, :], 0.0)

    srcs = devs // CORES
    pick_src = jnp.where(iota((srcs, devs), 1) == CORES * iota((srcs, devs), 0) + core, 1.0, 0.0).astype(BF16)
    pick_exp = jnp.where(iota((experts, LANE), 0) == chip * exp_chip + iota((experts, LANE), 1), 1.0, 0.0).astype(BF16)
    for src, dst in ((start_b, start_ref), (kept_b, cnt_ref)):
        part = jnp.dot(pick_src, src, preferred_element_type=F32).astype(BF16)
        dst[...] = jnp.dot(part, pick_exp, preferred_element_type=F32).astype(I32)


def send_kernel(size, row_ref, x_ref, out_ref, tok, rows3, stage, sem):
    tokens, d_model = x_ref.shape
    lanes = out_ref.shape[0]
    block = 16

    def fill(i, c):
        for u in range(8):
            t = i * 8 + u
            tok[row_ref[0, t]] = t
            tok[row_ref[1, t]] = t
        return c
    lax.fori_loop(0, tokens // 8, fill, 0)

    def relayout(i, c):
        r = pl.ds(pl.multiple_of(i * block, block), block)
        rows3[r] = x_ref[r].astype(F32).reshape(block, SUB, LANE).astype(BF16)
        return c
    lax.fori_loop(0, tokens // block, relayout, 0)

    slots = stage.shape[0]

    def copy(lane, slot):
        return pltpu.make_async_copy(stage.at[slot], out_ref.at[lane], sem.at[slot])

    def lane_step(lane, c):
        slot = lane % slots

        @pl.when(lane >= slots)
        def _():
            copy(lane - slots, slot).wait()

        def rows(i, c2):
            for u in range(8):
                r = i * 8 + u
                t = jnp.clip(tok[lane * size + r], 0, tokens - 1)
                stage[slot, r] = rows3[t]
            return c2
        lax.fori_loop(0, size // 8, rows, 0)
        copy(lane, slot).start()
        return c
    lax.fori_loop(0, lanes, lane_step, 0)
    for k in range(min(slots, lanes)):
        lane = lanes - min(slots, lanes) + k
        copy(lane, lane % slots).wait()


def ffn_kernel(size, cap_slot, start_ref, cnt_ref, core_ref, recv_ref, w1o, w1p, w2o, w2p, out_ref,
               recv_v, ret_v, w1_v, w2_v, xe, ze, x2, recv_sem, w_sem, out_sem):
    srcs = recv_ref.shape[0]
    exp_dev = w1o.shape[0]
    exp_chip = CORES * exp_dev
    core = core_ref[0]
    block = x2.shape[0]

    def recv_copy(s):
        return pltpu.make_async_copy(recv_ref.at[s], recv_v.at[pl.ds(s * size, size)], recv_sem.at[s])

    def out_copy(s):
        return pltpu.make_async_copy(ret_v.at[s, pl.ds(0, size)], out_ref.at[s], out_sem.at[s])

    def w_start(i):
        slot = i % 2
        local = i % exp_dev

        @pl.when(i // exp_dev == core)
        def _():
            pltpu.make_async_copy(w1o.at[local], w1_v.at[slot], w_sem.at[0, slot]).start()
            pltpu.make_async_copy(w2o.at[local], w2_v.at[slot], w_sem.at[1, slot]).start()

        @pl.when(i // exp_dev != core)
        def _():
            pltpu.make_async_copy(w1p.at[local], w1_v.at[slot], w_sem.at[0, slot]).start()
            pltpu.make_async_copy(w2p.at[local], w2_v.at[slot], w_sem.at[1, slot]).start()

    def w_wait(i):
        slot = i % 2
        pltpu.make_async_copy(w1o.at[0], w1_v.at[slot], w_sem.at[0, slot]).wait()
        pltpu.make_async_copy(w2o.at[0], w2_v.at[slot], w_sem.at[1, slot]).wait()

    for s in range(srcs):
        recv_copy(s).start()
    w_start(jnp.int32(0))
    for s in range(srcs):
        recv_copy(s).wait()

    def expert(i, c):
        slot = i % 2

        @pl.when(i + 1 < exp_chip)
        def _():
            w_start(i + 1)

        def gather(s, pos):
            n = cnt_ref[s, i]

            @pl.when(n > 0)
            def _():
                a = s * size + start_ref[s, i]
                for j in range(cap_slot):
                    xe[pos + j] = recv_v[a + j]
            return pos + n
        total = lax.fori_loop(0, srcs, gather, jnp.int32(0))
        w_wait(i)

        def tile(b, c2):
            base = pl.multiple_of(b * block, block)
            for q in range(block // 16):
                v = xe[pl.ds(base + q * 16, 16)].astype(F32).reshape(16, SUB * LANE)
                x2[pl.ds(q * 16, 16), :] = v.astype(BF16)
            h = jnp.dot(x2[...], w1_v[slot], preferred_element_type=F32)
            h = jax.nn.gelu(h, approximate=True).astype(BF16)
            z = jnp.dot(h, w2_v[slot], preferred_element_type=F32).astype(BF16).astype(F32)
            ze[pl.ds(base, block)] = z.reshape(block, SUB, LANE).astype(BF16)
            return c2
        lax.fori_loop(0, (total + block - 1) // block, tile, 0)

        def scatter(s, pos):
            n = cnt_ref[s, i]

            @pl.when(n > 0)
            def _():
                a = start_ref[s, i]
                for j in range(cap_slot):
                    ret_v[s, a + j] = ze[pos + j]
            return pos + n
        lax.fori_loop(0, srcs, scatter, jnp.int32(0))
        return c
    lax.fori_loop(0, exp_chip, expert, 0)
    for s in range(srcs):
        out_copy(s).start()
    for s in range(srcs):
        out_copy(s).wait()


def combine_kernel(row_ref, gate_ref, x_ref, ret_ref, out_ref, ret_v, y3, sem):
    tokens, d_model = x_ref.shape
    lanes, size = ret_ref.shape[:2]
    last = lanes * size - 1
    block = 16

    def copy(s):
        return pltpu.make_async_copy(ret_ref.at[s], ret_v.at[pl.ds(s * size, size)], sem.at[s])
    for s in range(lanes):
        copy(s).start()
    for s in range(lanes):
        copy(s).wait()

    def step(i, c):
        base = pl.multiple_of(i * block, block)
        for u in range(block):
            t = base + u
            g1 = gate_ref[0, t]
            g2 = gate_ref[1, t]
            z1 = ret_v[jnp.minimum(row_ref[0, t], last)].astype(F32)
            z2 = ret_v[jnp.minimum(row_ref[1, t], last)].astype(F32)
            y3[u] = jnp.where(g1 > 0, g1 * z1, 0.0) + jnp.where(g2 > 0, g2 * z2, 0.0)
        r = pl.ds(base, block)
        y = y3[...].reshape(block, d_model)
        out_ref[r, :] = (x_ref[r, :].astype(F32) + y).astype(BF16)
        return c
    lax.fori_loop(0, tokens // block, step, 0)


def spec(space):
    return pl.BlockSpec(memory_space=space)


SMEM = pltpu.SMEM
VMEM = pltpu.VMEM
ANY = pl.ANY


def params():
    return pltpu.CompilerParams(vmem_limit_bytes=VMEM_LIMIT)


def solution(mesh):
    devs = mesh.shape['ep']
    row_spec = P(('dp', 'ep'), None)
    expert_spec = P('ep', None, None)
    groups = [[i for i in range(devs) if i % CORES == c] for c in range(CORES)]
    partner = [(i, i ^ 1) for i in range(devs)]

    def local_step(x_rows, logits, w_in, w_out):
        tokens, d_model = x_rows.shape
        experts = logits.shape[1]
        exp_dev, _, hidden = w_in.shape
        capacity = CAP_FACTOR * tokens * devs // experts
        cap_slot = SLOT_FACTOR * tokens // experts
        exp_chip = CORES * exp_dev
        chips = devs // CORES
        full = exp_chip * cap_slot
        sizes = tuple(full * k // 32 for k in (21, 23, 32))
        me = lax.axis_index('ep').astype(I32)

        tok, gate, count = pl.pallas_call(
            route_kernel, name='route',
            out_shape=(jax.ShapeDtypeStruct((8, tokens), I32), jax.ShapeDtypeStruct((8, tokens), F32),
                       jax.ShapeDtypeStruct((8, experts), F32)),
            compiler_params=params())(logits)
        counts = lax.all_gather(count[0], 'ep')
        row, keep, start, cnt, pick = pl.pallas_call(
            functools.partial(plan_kernel, sizes, capacity, exp_dev), name='plan',
            out_shape=(jax.ShapeDtypeStruct((8, tokens), I32), jax.ShapeDtypeStruct((8, tokens), F32),
                       jax.ShapeDtypeStruct((chips, LANE), I32), jax.ShapeDtypeStruct((chips, LANE), I32),
                       jax.ShapeDtypeStruct((8, LANE), I32)),
            in_specs=[spec(SMEM)] + [spec(VMEM)] * 3,
            compiler_params=params())(me.reshape(1), counts, tok, gate)
        core = (me % CORES).reshape(1)

        def branch(size, x_rows, w_in, w_out, row, keep, start, cnt, core):
            lane_shape = jax.ShapeDtypeStruct((chips, size, SUB, LANE), BF16)
            w_in_p = lax.ppermute(w_in, 'ep', partner)
            w_out_p = lax.ppermute(w_out, 'ep', partner)
            send = pl.pallas_call(
                functools.partial(send_kernel, size), name='send', out_shape=lane_shape,
                in_specs=[spec(SMEM), spec(VMEM)], out_specs=spec(ANY),
                scratch_shapes=[SMEM((chips * size + 8,), I32), VMEM((tokens, SUB, LANE), BF16),
                                VMEM((4, size, SUB, LANE), BF16), pltpu.SemaphoreType.DMA((4,))],
                compiler_params=params())(row, x_rows)
            recv = lax.all_to_all(send, 'ep', 0, 0, axis_index_groups=groups, tiled=True)
            rows_max = capacity + cap_slot
            ret = pl.pallas_call(
                functools.partial(ffn_kernel, size, cap_slot), name='ffn', out_shape=lane_shape,
                in_specs=[spec(SMEM)] * 3 + [spec(ANY)] * 5, out_specs=spec(ANY),
                scratch_shapes=[
                    VMEM((chips * size + cap_slot, SUB, LANE), BF16),
                    VMEM((chips, size + cap_slot, SUB, LANE), BF16),
                    VMEM((2, d_model, hidden), BF16), VMEM((2, hidden, d_model), BF16),
                    VMEM((rows_max, SUB, LANE), BF16), VMEM((rows_max, SUB, LANE), BF16),
                    VMEM((LANE, d_model), BF16),
                    pltpu.SemaphoreType.DMA((chips,)), pltpu.SemaphoreType.DMA((2, 2)),
                    pltpu.SemaphoreType.DMA((chips,))],
                cost_estimate=pl.CostEstimate(flops=4 * chips * size * d_model * hidden,
                                              bytes_accessed=8 * exp_dev * d_model * hidden, transcendentals=0),
                compiler_params=params())(start, cnt, core, recv, w_in, w_in_p, w_out, w_out_p)
            back = lax.all_to_all(ret, 'ep', 0, 0, axis_index_groups=groups, tiled=True)
            return pl.pallas_call(
                combine_kernel, name='combine', out_shape=jax.ShapeDtypeStruct((tokens, d_model), BF16),
                in_specs=[spec(SMEM)] * 2 + [spec(VMEM), spec(ANY)], out_specs=spec(VMEM),
                scratch_shapes=[VMEM((chips * size, SUB, LANE), BF16), VMEM((16, SUB, LANE), F32),
                                pltpu.SemaphoreType.DMA((chips,))],
                compiler_params=params())(row, keep, x_rows, back)

        branches = [functools.partial(branch, size) for size in sizes]
        return lax.switch(pick[0, 0], branches, x_rows, w_in, w_out, row, keep, start, cnt, core)

    return jax.shard_map(local_step, mesh=mesh, in_specs=(row_spec, row_spec, expert_spec, expert_spec),
                         out_specs=row_spec, check_vma=False)
```

time: 940 us -> 427 us (0.45)
  the two profiles are of different devices: /device:TPU:107 before, /device:TPU:104 now
where the time goes in v1:
time: 427 us; the launch traced here: 422 us
  blocking collectives  166 us (39%)
  waiting for transfers between devices  163 us (38%)
  Pallas kernels  83.1 us (19%)
  starting transfers between devices  7.7 us (2%)
    all_to_all x1, waiting for transfers between devices, branch(): lax.all_to_all(send, 'ep', 0, 0, axis_index_groups=groups, tiled=True)  163 us
    all_to_all x1, blocking collectives, branch(): back = lax.all_to_all(ret, 'ep', 0, 0, axis_index_groups=groups, tiled=True)  131 us
    pallas_call x1, Pallas kernels, branch(): pl.pallas_call(functools.partial(ffn_kernel, size, cap_slot), name='ffn',...  42.7 us
    all_gather x1, blocking collectives, local_step(): counts = lax.all_gather(count[0], 'ep')  34.2 us
    pallas_call x1, Pallas kernels, branch(): pl.pallas_call(functools.partial(send_kernel, size), name='send', out_sha...  18.1 us
    pallas_call x1, Pallas kernels, branch(): pl.pallas_call(combine_kernel, name='combine', out_shape=jax.ShapeDtypeSt...  16.9 us
  transfers between devices with their start and end apart: 3, of which 1 were waited for; matrix products, arithmetic and copies ran while one was open for 0% of the time, Pallas kernels for 0%

profile of v1, /device:TPU:104, one launch (start us, length us, event | category | flops | bytes accessed | tf_op | source)
XLA Modules:
  0.0 422.5 jit_solution(10836622670918818305)
XLA Ops:
  0.0 3.6 route.1
  3.6 0.7 slice_bitcast_fusion
  4.3 34.2 %all-gather = f32[32,1,256]{2,1,0:T(1,128)S(1)} all-gather(f32[1,1,256]{2,1,0:T(1,128)S(1)} %slice_bitcast_fusion), channel_id=1, replica_groups=mesh['dp'=1,'ep'=32] {'ep'}, dimensions={0}, use_global_device_ids=true | all-gather | bytes 33792 | tf_op jit(solution)/shard_map/all_gather | solution.py:304
  38.5 0.6 copy.19
  39.2 1.7 plan.1
  40.9 1.2 slice.7
  42.7 379.8 %conditional.1 = (bf16[1024,2048]{1,0:T(8,128)(2,1)}) conditional(s32[]{:T(128)} %bitcast.5, (s32[8,1024]{1,0:T(8,128)S(1)}, bf16[1024,2048]{1,0:T(8,128)(2,1)}, bf16[8,2048,512]{2,1,0:T(8,128)(2,1)}, bf16[8,512,2048]{2,1,0:T(8,128)(2,1)}, s32[16,128]{1,0:T(8,128)S(1)}, /*index=5*/s32[16,128]{1,0:T(8,128)S(1)}, pred[]{:T(512)}, ...), branch_computations={%region_0.1_spmd, %region_1.2_spmd, %region_2.3_spmd} | conditional | flops 17179869184 | bytes 285212864 | solution.py:349
  42.7 0.1 collective-permute-start
  42.9 0.5 collective-permute-start.1
  43.3 18.1 %send.3 = bf16[16,168,16,128]{3,2,1,0:T(8,128)(2,1)} custom-call(s32[8,1024]{1,0:T(8,128)S(1)} %get-tuple-element.56.row_ref, bf16[1024,2048]{1,0:T(8,128)(2,1)} %get-tuple-element.110.x_ref), custom_call_target="tpu_custom_call" | custom-call | tf_op jit(solution)/shard_map/cond/branch_0_fun/send/pallas_call | solution.py:318
  61.4 7.1 %all-to-all-start = ((bf16[16,168,16,128]{3,2,1,0:T(8,128)(2,1)}), bf16[16,168,16,128]{3,2,1,0:T(8,128)(2,1)}, u32[]{:S(2)}, u32[]{:S(2)}) async-start(bf16[16,168,16,128]{3,2,1,0:T(8,128)(2,1)} %send.3), calls=%async_computation | async-start | bytes 22020096 | tf_op jit(solution)/shard_map/cond/branch_0_fun/all_to_all | solution.py:324
  68.5 162.9 %all-to-all-done.recv_ref = bf16[16,168,16,128]{3,2,1,0:T(8,128)(2,1)} async-done(((bf16[16,168,16,128]{3,2,1,0:T(8,128)(2,1)}), bf16[16,168,16,128]{3,2,1,0:T(8,128)(2,1)}, u32[]{:S(2)}, u32[]{:S(2)}) %all-to-all-start) | async-done | bytes 11010080 | tf_op jit(solution)/shard_map/cond/branch_0_fun/all_to_all | solution.py:324
  231.5 0.0 collective-permute-done.w1p
  231.5 0.0 collective-permute-done.1.w2p
  231.5 42.7 %ffn.3 = bf16[16,168,16,128]{3,2,1,0:T(8,128)(2,1)} custom-call(s32[16,128]{1,0:T(8,128)S(1)} %get-tuple-element.60.start_ref, s32[16,128]{1,0:T(8,128)S(1)} %get-tuple-element.61.cnt_ref, s32[1]{0:T(128)} %bitcast.core_ref, bf16[16,168,16,128]{3,2,1,0:T(8,128)(2,1)} %all-to-all-done.recv_ref, bf16[8,2048,512]{2,1,0:T(8,128)(2,1)} %get-tuple-element.113.w1o, ...), custom_call_target="tpu_custom_call" | custom-call | flops 11274289152 | bytes 67108864 | tf_op jit(solution)/shard_map/cond/branch_0_fun/ffn/pallas_call | solution.py:326
  274.2 131.3 %all_to_all.24.ret_ref = bf16[16,168,16,128]{3,2,1,0:T(8,128)(2,1)} all-to-all(bf16[16,168,16,128]{3,2,1,0:T(8,128)(2,1)} %ffn.3), channel_id=1, replica_groups={{0,2,4,6,8,10,12,14,16,18,20,22,24,26,28,30},{1,3,5,7,9,11,13,15,17,19,..., dimensions={0} | all-to-all | bytes 22020096 | tf_op jit(solution)/shard_map/cond/branch_0_fun/all_to_all | solution.py:340
  405.6 16.9 %combine.3 = bf16[1024,2048]{1,0:T(8,128)(2,1)} custom-call(s32[8,1024]{1,0:T(8,128)S(1)} %get-tuple-element.56.row_ref, f32[8,1024]{1,0:T(8,128)S(1)} %get-tuple-element.58.gate_ref, bf16[1024,2048]{1,0:T(8,128)(2,1)} %get-tuple-element.110.x_ref, bf16[16,168,16,128]{3,2,1,0:T(8,128)(2,1)} %all_to_all.24.ret_ref), custom_call_target="tpu_custom_call" | custom-call | tf_op jit(solution)/shard_map/cond/branch_0_fun/combine/pallas_call | solution.py:341
Async XLA Ops:
  42.7 188.7 %collective-permute-start = (bf16[8,2048,512]{2,1,0:T(8,128)(2,1)}, bf16[8,2048,512]{2,1,0:T(8,128)(2,1)}, u32[]{:S(2)}, u32[]{:S(2)}) collective-permute-start(bf16[8,2048,512]{2,1,0:T(8,128)(2,1)} %get-tuple-element.113.w1o), channel_id=1, source_target_pairs={{0,1},{1,0},{2,3},{3,2},{4,5},{5,4},{6,7},{7,6},{8,9},{9,8},{10,11... | collective-permute-start | bytes 50331656 | tf_op jit(solution)/shard_map/cond/branch_0_fun/ppermute | solution.py:316
  42.9 188.6 %collective-permute-start.1 = (bf16[8,512,2048]{2,1,0:T(8,128)(2,1)}, bf16[8,512,2048]{2,1,0:T(8,128)(2,1)}, u32[]{:S(2)}, u32[]{:S(2)}) collective-permute-start(bf16[8,512,2048]{2,1,0:T(8,128)(2,1)} %get-tuple-element.116.w2o), channel_id=1, source_target_pairs={{0,1},{1,0},{2,3},{3,2},{4,5},{5,4},{6,7},{7,6},{8,9},{9,8},{10,11... | collective-permute-start | bytes 50331656 | tf_op jit(solution)/shard_map/cond/branch_0_fun/ppermute | solution.py:317
  61.4 170.0 %all-to-all-start = ((bf16[16,168,16,128]{3,2,1,0:T(8,128)(2,1)}), bf16[16,168,16,128]{3,2,1,0:T(8,128)(2,1)}, u32[]{:S(2)}, u32[]{:S(2)}) async-start(bf16[16,168,16,128]{3,2,1,0:T(8,128)(2,1)} %send.3), calls=%async_computation | async-start | bytes 22020096 | tf_op jit(solution)/shard_map/cond/branch_0_fun/all_to_all | solution.py:324
